TPU v7x, 32 devices: a whole 2x2x4 slice. The times are simulated.
32 devices in a mesh: dp: 2 (over core), seq: 16 (over z, y, x).
Axes of the slice: x: 2, y: 2, z: 4, core: 2. Of those that a mesh axis runs over, the one named last changes fastest.
Arguments:
- latent: bfloat16 [32, 1024, 1152], P(('dp', 'seq')), parts along dimension 0, may hold values from -6 to 6
- w_qkv_space: bfloat16 [1152, 1728], replicated, may hold values from -0.1875 to 0.1875
- w_out_space: bfloat16 [576, 1152], replicated, may hold values from -0.25 to 0.25
- w_qkv_time: bfloat16 [1152, 1728], replicated, may hold values from -0.1875 to 0.1875
- w_out_time: bfloat16 [576, 1152], replicated, may hold values from -0.25 to 0.25
- modulation: float32 [12, 1152], P('dp'), parts along dimension 0, may hold values from -1.5 to 5
Outputs:
- block_out: bfloat16 [32, 1024, 1152], P(('dp', 'seq')), parts along dimension 0
There are 2 independent parts, one for each index of `dp`. A program takes and returns all parts, laid end to end along the dimension named above; an argument that names none is the same for every part. Nothing has to cross between parts.
All inputs are finite; a program needn't handle non-finite values.
Results may differ from a plain program's by a relative error of at most 0.02.
The roundings to bfloat16 on the way count: a program that leaves them out, or rounds other values in their place, can miss the bound.
Values may be sent and summed in bfloat16 or wider, within the bound.
No kernel may reach another device: no remote copies, remote signals or barrier semaphores. Data moves between devices by JAX's collectives and lax.ppermute only.
A program may use at most 128 MiB of HBM per device.

v0:
```python
import functools
import math

import jax
import jax.numpy as jnp
from jax import lax
from jax.experimental import pallas as pl
from jax.experimental.pallas import tpu as pltpu
from jax.sharding import PartitionSpec as P

HEADS = 8
HEAD_DIM = 72
EPS = 1e-06
CHUNKS = 2
ROWS = 256
INNER = HEADS * HEAD_DIM
POWER = math.log2(math.e) / math.sqrt(HEAD_DIM)
LIMIT = 20 * 1024 * 1024


def mixed_rows(rows, modulation, first):
    values = rows.astype(jnp.float32)
    centred = values - jnp.mean(values, -1, keepdims=True)
    spread = jnp.mean(centred * centred, -1, keepdims=True)
    normed = centred * lax.rsqrt(spread + EPS)
    return (normed * (1.0 + modulation[first + 1]) + modulation[first]).astype(jnp.bfloat16)


def rows_by_columns(rows, w_t):
    product = lax.dot_general(rows, w_t, (((1,), (1,)), ((), ())), preferred_element_type=jnp.float32)
    return product.astype(jnp.bfloat16)


def project_kernel(rows_ref, w_ref, mod_ref, out_ref):
    mixed = mixed_rows(rows_ref[...], mod_ref[...], 0)
    out_ref[...] = rows_by_columns(mixed, w_ref[...])


def attend(query, key, value, keep=None):
    scores = lax.dot_general(query, key, (((1,), (1,)), ((), ())), preferred_element_type=jnp.float32)
    if keep is not None:
        scores = jnp.where(keep, scores, -jnp.inf)
    top = jnp.max(scores, 1, keepdims=True)
    expo = jnp.exp2((scores - top) * POWER)
    total = jnp.sum(expo, 1, keepdims=True)
    out = jnp.dot(expo.astype(jnp.bfloat16), value, preferred_element_type=jnp.float32)
    return (out / total).astype(jnp.bfloat16)


def head_columns(kind, head):
    start = kind * INNER + head * HEAD_DIM
    return slice(start, start + HEAD_DIM)


def space_kernel(rows_ref, query_ref, triple_ref, w_out_ref, mod_ref, out_ref, heads_ref):
    for head in range(HEADS):
        heads_ref[:, head_columns(0, head)] = attend(
            query_ref[:, head_columns(0, head)],
            triple_ref[:, head_columns(1, head)],
            triple_ref[:, head_columns(2, head)],
        )
    delta = jnp.dot(heads_ref[...], w_out_ref[...], preferred_element_type=jnp.float32)
    out_ref[...] = (rows_ref[...].astype(jnp.float32) + mod_ref[2] * delta).astype(jnp.bfloat16)


def time_kernel(rows_ref, w_ref, mod_ref, out_ref, triple_ref, heads_ref):
    members, positions, width = rows_ref.shape
    tokens = members * positions
    rows = rows_ref[...].astype(jnp.float32).reshape(tokens, width)
    triple_ref[...] = rows_by_columns(mixed_rows(rows, mod_ref[...], 3), w_ref[...])
    left = lax.broadcasted_iota(jnp.int32, (tokens, tokens), 0)
    right = lax.broadcasted_iota(jnp.int32, (tokens, tokens), 1)
    keep = lax.rem(left, positions) == lax.rem(right, positions)
    for head in range(HEADS):
        heads_ref[:, head_columns(0, head)] = attend(
            triple_ref[:, head_columns(0, head)],
            triple_ref[:, head_columns(1, head)],
            triple_ref[:, head_columns(2, head)],
            keep,
        )
    done = heads_ref[...].astype(jnp.float32).reshape(members, positions, INNER)
    out_ref[...] = done.astype(jnp.bfloat16)


def finish_kernel(rows_ref, heads_ref, w_out_ref, mod_ref, *refs):
    delta = jnp.dot(heads_ref[...], w_out_ref[...], preferred_element_type=jnp.float32)
    refs[-1][...] = (rows_ref[...].astype(jnp.float32) + mod_ref[5] * delta).astype(jnp.bfloat16)


def whole(array):
    return pl.BlockSpec(array.shape, lambda i: (0,) * array.ndim)


def params():
    return pltpu.CompilerParams(vmem_limit_bytes=LIMIT)


def project(frame, w_t, modulation):
    tokens, width = frame.shape
    columns = w_t.shape[0]
    return pl.pallas_call(
        project_kernel,
        grid=(tokens // ROWS,),
        in_specs=[pl.BlockSpec((ROWS, width), lambda i: (i, 0)), whole(w_t), whole(modulation)],
        out_specs=pl.BlockSpec((ROWS, columns), lambda i: (i, 0)),
        out_shape=jax.ShapeDtypeStruct((tokens, columns), jnp.bfloat16),
        compiler_params=params(),
        cost_estimate=pl.CostEstimate(flops=2 * tokens * width * columns, transcendentals=0, bytes_accessed=10000000),
        name="project",
    )(frame, w_t, modulation)


def space_chunk(frame, triple, w_out, modulation, chunk):
    tokens, width = frame.shape
    block = tokens // CHUNKS
    steps = block // ROWS
    return pl.pallas_call(
        space_kernel,
        grid=(steps,),
        in_specs=[
            pl.BlockSpec((ROWS, width), lambda i: (chunk * steps + i, 0)),
            pl.BlockSpec((ROWS, triple.shape[1]), lambda i: (chunk * steps + i, 0)),
            whole(triple),
            whole(w_out),
            whole(modulation),
        ],
        out_specs=pl.BlockSpec((ROWS, width), lambda i: (i, 0)),
        out_shape=jax.ShapeDtypeStruct((block, width), jnp.bfloat16),
        scratch_shapes=[pltpu.VMEM((ROWS, INNER), jnp.bfloat16)],
        compiler_params=params(),
        cost_estimate=pl.CostEstimate(flops=6 * block * tokens * 256 * HEADS, transcendentals=HEADS * block * tokens, bytes_accessed=6000000),
        name="space",
    )(frame, triple, triple, w_out, modulation)


def time_chunk(patches, w_t, modulation, members):
    tokens, width = patches.shape
    positions = tokens // members
    some = min(positions, max(8, ROWS // members))
    columns = w_t.shape[0]
    heads = pl.pallas_call(
        time_kernel,
        grid=(positions // some,),
        in_specs=[pl.BlockSpec((members, some, width), lambda i: (0, i, 0)), whole(w_t), whole(modulation)],
        out_specs=pl.BlockSpec((members, some, INNER), lambda i: (0, i, 0)),
        out_shape=jax.ShapeDtypeStruct((members, positions, INNER), jnp.bfloat16),
        scratch_shapes=[pltpu.VMEM((members * some, columns), jnp.bfloat16), pltpu.VMEM((members * some, INNER), jnp.bfloat16)],
        compiler_params=params(),
        cost_estimate=pl.CostEstimate(flops=4 * tokens * width * columns, transcendentals=HEADS * tokens * tokens, bytes_accessed=5000000),
        name="time",
    )(patches.reshape(members, positions, width), w_t, modulation)
    return heads.reshape(tokens, INNER)


def finish_chunk(rows, heads, w_out, modulation, chunk, earlier):
    block, width = rows.shape
    steps = block // ROWS
    extra = [] if earlier is None else [earlier]
    return pl.pallas_call(
        finish_kernel,
        grid=(steps,),
        in_specs=[
            pl.BlockSpec((ROWS, width), lambda i: (i, 0)),
            pl.BlockSpec((ROWS, INNER), lambda i: (i, 0)),
            whole(w_out),
            whole(modulation),
        ]
        + [pl.BlockSpec(memory_space=pl.ANY) for _ in extra],
        out_specs=pl.BlockSpec((ROWS, width), lambda i: (chunk * steps + i, 0)),
        out_shape=jax.ShapeDtypeStruct((block * CHUNKS, width), jnp.bfloat16),
        input_output_aliases={4: 0} if extra else {},
        compiler_params=params(),
        cost_estimate=pl.CostEstimate(flops=2 * block * width * INNER, transcendentals=0, bytes_accessed=4000000),
        name="finish",
    )(rows, heads, w_out, modulation, *extra)


def exchange(array):
    return lax.all_to_all(array, "seq", split_axis=0, concat_axis=0, tiled=True)


def shards(latent, w_qkv_space, w_out_space, w_qkv_time, w_out_time, modulation):
    members = lax.axis_size("seq")
    frame = latent[0]
    triple = project(frame, w_qkv_space.T, modulation)
    rows = [space_chunk(frame, triple, w_out_space, modulation, chunk) for chunk in range(CHUNKS)]
    patches = [exchange(part) for part in rows]
    heads = [exchange(time_chunk(part, w_qkv_time.T, modulation, members)) for part in patches]
    done = None
    for chunk in range(CHUNKS):
        done = finish_chunk(rows[chunk], heads[chunk], w_out_time, modulation, chunk, done)
    return done[None]


def solution(mesh):
    in_specs = (P(("dp", "seq"), None, None), P(), P(), P(), P(), P("dp", None))
    out_specs = P(("dp", "seq"), None, None)
    return jax.shard_map(shards, mesh=mesh, in_specs=in_specs, out_specs=out_specs, check_vma=False)
```

profile of v0, /device:TPU:0, one launch (start us, length us, event | category | flops | bytes accessed | tf_op | source)
XLA Modules:
  0.0 141.8 jit_solution(7369150996098264481)
XLA Ops:
  0.0 0.8 copy-done.3
  0.8 2.1 %copy-done.5 = bf16[1152,1728]{0,1:T(8,128)(2,1)S(1)} copy-done((bf16[1152,1728]{0,1:T(8,128)(2,1)S(1)}, bf16[1152,1728]{0,1:T(8,128)(2,1)}, u32[]{:S(2)}) %copy-start.5) | copy-done | bytes 3981336
  2.9 1.7 %copy-done.8 = bf16[1,1024,1152]{2,1,0:T(8,128)(2,1)S(1)} copy-done((bf16[1,1024,1152]{2,1,0:T(8,128)(2,1)S(1)}, bf16[1,1024,1152]{2,1,0:T(8,128)(2,1)}, u32[]{:S(2)}) %copy-start.8) | copy-done | bytes 2359320
  4.6 6.6 %project.1.query_ref.triple_ref = bf16[1024,1728]{1,0:T(8,128)(2,1)S(1)} custom-call(bf16[1024,1152]{1,0:T(8,128)(2,1)S(1)} %bitcast.13, bf16[1728,1152]{1,0:T(8,128)(2,1)S(1)} %bitcast.10, f32[6,1152]{1,0:T(8,128)S(1)} %copy-done.3), custom_call_target="tpu_custom_call" | custom-call | flops 4076863488 | bytes 10000000 | tf_op jit(solution)/shard_map/project/pallas_call | solution.py:101
  11.2 15.6 %space.3.rows_ref = bf16[512,1152]{1,0:T(8,128)(2,1)} custom-call(bf16[1024,1152]{1,0:T(8,128)(2,1)S(1)} %bitcast.14, bf16[1024,1728]{1,0:T(8,128)(2,1)S(1)} %project.1.query_ref.triple_ref, bf16[1024,1728]{1,0:T(8,128)(2,1)S(1)} %project.1.query_ref.triple_ref, bf16[576,1152]{1,0:T(8,128)(2,1)S(1)} %copy-done.10, f32[6,1152]{1,0:T(8,128)S(1)} %copy-done.4), custom_call_target="tpu_custom_call" | custom-call | flops 6442450944 | bytes 6000000 | tf_op jit(solution)/shard_map/space/pallas_call | solution.py:117
  26.8 8.4 %all-to-all-start.2 = ((bf16[16,32,1152]{2,1,0:T(8,128)(2,1)}), bf16[16,32,1152]{2,1,0:T(8,128)(2,1)S(1)}, u32[]{:S(2)}, u32[]{:S(2)}) async-start(bf16[16,32,1152]{2,1,0:T(8,128)(2,1)} %bitcast.5), calls=%async_computation.2 | async-start | bytes 2359296 | tf_op jit(solution)/shard_map/all_to_all | solution.py:179
  35.2 1.7 %copy-done.9 = bf16[1,1024,1152]{2,1,0:T(8,128)(2,1)S(1)} copy-done((bf16[1,1024,1152]{2,1,0:T(8,128)(2,1)S(1)}, bf16[1,1024,1152]{2,1,0:T(8,128)(2,1)}, u32[]{:S(2)}) %copy-start.9) | copy-done | bytes 2359320
  36.9 2.0 %copy-done.12 = bf16[1024,1728]{1,0:T(8,128)(2,1)S(1)} copy-done((bf16[1024,1728]{1,0:T(8,128)(2,1)S(1)}, bf16[1024,1728]{1,0:T(8,128)(2,1)}, u32[]{:S(2)}) %copy-start.12) | copy-done | bytes 3538968
  38.9 15.4 %space.2.rows_ref = bf16[512,1152]{1,0:T(8,128)(2,1)} custom-call(bf16[1024,1152]{1,0:T(8,128)(2,1)S(1)} %bitcast.15, bf16[1024,1728]{1,0:T(8,128)(2,1)S(1)} %copy-done.12, bf16[1024,1728]{1,0:T(8,128)(2,1)S(1)} %copy-done.12, bf16[576,1152]{1,0:T(8,128)(2,1)S(1)} %copy-done.10, f32[6,1152]{1,0:T(8,128)S(1)} %copy-done.4), custom_call_target="tpu_custom_call" | custom-call | flops 6442450944 | bytes 6000000 | tf_op jit(solution)/shard_map/space/pallas_call | solution.py:117
  54.3 7.8 %all-to-all-done.2.rows_ref = bf16[16,32,1152]{2,1,0:T(8,128)(2,1)S(1)} async-done(((bf16[16,32,1152]{2,1,0:T(8,128)(2,1)}), bf16[16,32,1152]{2,1,0:T(8,128)(2,1)S(1)}, u32[]{:S(2)}, u32[]{:S(2)}) %all-to-all-start.2) | async-done | bytes 1179680 | tf_op jit(solution)/shard_map/all_to_all | solution.py:179
  62.1 6.2 %all-to-all-start = ((bf16[16,32,1152]{2,1,0:T(8,128)(2,1)}), bf16[16,32,1152]{2,1,0:T(8,128)(2,1)S(1)}, u32[]{:S(2)}, u32[]{:S(2)}) async-start(bf16[16,32,1152]{2,1,0:T(8,128)(2,1)} %bitcast.2), calls=%async_computation | async-start | bytes 2359296 | tf_op jit(solution)/shard_map/all_to_all | solution.py:179
  68.3 2.1 %copy-done.6 = bf16[1152,1728]{0,1:T(8,128)(2,1)S(1)} copy-done((bf16[1152,1728]{0,1:T(8,128)(2,1)S(1)}, bf16[1152,1728]{0,1:T(8,128)(2,1)}, u32[]{:S(2)}) %copy-start.6) | copy-done | bytes 3981336
  70.5 10.7 %time.3 = bf16[16,32,576]{2,1,0:T(8,128)(2,1)} custom-call(bf16[16,32,1152]{2,1,0:T(8,128)(2,1)S(1)} %all-to-all-done.2.rows_ref, bf16[1728,1152]{1,0:T(8,128)(2,1)S(1)} %bitcast.11, f32[6,1152]{1,0:T(8,128)S(1)} %copy-done.4), custom_call_target="tpu_custom_call" | custom-call | flops 4076863488 | bytes 5000000 | tf_op jit(solution)/shard_map/time/pallas_call | solution.py:141
  81.1 13.0 %all-to-all-done.rows_ref = bf16[16,32,1152]{2,1,0:T(8,128)(2,1)S(1)} async-done(((bf16[16,32,1152]{2,1,0:T(8,128)(2,1)}), bf16[16,32,1152]{2,1,0:T(8,128)(2,1)S(1)}, u32[]{:S(2)}, u32[]{:S(2)}) %all-to-all-start) | async-done | bytes 1179680 | tf_op jit(solution)/shard_map/all_to_all | solution.py:179
  94.1 1.0 copy-done.1
  95.1 6.1 %all-to-all-start.3 = ((bf16[16,32,576]{2,1,0:T(8,128)(2,1)}), bf16[16,32,576]{2,1,0:T(8,128)(2,1)S(1)}, u32[]{:S(2)}, u32[]{:S(2)}) async-start(bf16[16,32,576]{2,1,0:T(8,128)(2,1)} %time.3), calls=%async_computation.3 | async-start | bytes 1310720 | tf_op jit(solution)/shard_map/all_to_all | solution.py:179
  101.3 1.3 copy-done.2
  102.5 2.1 %copy-done.7 = bf16[1152,1728]{0,1:T(8,128)(2,1)S(1)} copy-done((bf16[1152,1728]{0,1:T(8,128)(2,1)S(1)}, bf16[1152,1728]{0,1:T(8,128)(2,1)}, u32[]{:S(2)}) %copy-start.7) | copy-done | bytes 3981336
  104.6 10.7 %time.2 = bf16[16,32,576]{2,1,0:T(8,128)(2,1)} custom-call(bf16[16,32,1152]{2,1,0:T(8,128)(2,1)S(1)} %copy-done.2, bf16[1728,1152]{1,0:T(8,128)(2,1)S(1)} %bitcast.12, f32[6,1152]{1,0:T(8,128)S(1)} %copy-done.4), custom_call_target="tpu_custom_call" | custom-call | flops 4076863488 | bytes 5000000 | tf_op jit(solution)/shard_map/time/pallas_call | solution.py:141
  115.4 2.3 %all-to-all-done.3 = bf16[16,32,576]{2,1,0:T(8,128)(2,1)S(1)} async-done(((bf16[16,32,576]{2,1,0:T(8,128)(2,1)}), bf16[16,32,576]{2,1,0:T(8,128)(2,1)S(1)}, u32[]{:S(2)}, u32[]{:S(2)}) %all-to-all-start.3) | async-done | bytes 589856 | tf_op jit(solution)/shard_map/all_to_all | solution.py:179
  117.7 4.6 %all-to-all-start.1 = ((bf16[16,32,576]{2,1,0:T(8,128)(2,1)}), bf16[16,32,576]{2,1,0:T(8,128)(2,1)S(1)}, u32[]{:S(2)}, u32[]{:S(2)}) async-start(bf16[16,32,576]{2,1,0:T(8,128)(2,1)} %time.2), calls=%async_computation.1 | async-start | bytes 1310720 | tf_op jit(solution)/shard_map/all_to_all | solution.py:179
  122.3 3.2 %finish.2.refs_0_ = bf16[1024,1152]{1,0:T(8,128)(2,1)} custom-call(bf16[512,1152]{1,0:T(8,128)(2,1)} %space.3.rows_ref, bf16[512,576]{1,0:T(8,128)(2,1)S(1)} %bitcast.9, bf16[576,1152]{1,0:T(8,128)(2,1)S(1)} %copy-done, f32[6,1152]{1,0:T(8,128)S(1)} %copy-done.4), custom_call_target="tpu_custom_call" | custom-call | flops 679477248 | bytes 4000000 | tf_op jit(solution)/shard_map/finish/pallas_call | solution.py:159
  125.5 13.1 %all-to-all-done.1 = bf16[16,32,576]{2,1,0:T(8,128)(2,1)S(1)} async-done(((bf16[16,32,576]{2,1,0:T(8,128)(2,1)}), bf16[16,32,576]{2,1,0:T(8,128)(2,1)S(1)}, u32[]{:S(2)}, u32[]{:S(2)}) %all-to-all-start.1) | async-done | bytes 589856 | tf_op jit(solution)/shard_map/all_to_all | solution.py:179
  138.6 3.2 %finish.3 = bf16[1024,1152]{1,0:T(8,128)(2,1)} custom-call(bf16[512,1152]{1,0:T(8,128)(2,1)} %space.2.rows_ref, bf16[512,576]{1,0:T(8,128)(2,1)S(1)} %bitcast.8, bf16[576,1152]{1,0:T(8,128)(2,1)S(1)} %copy-done, f32[6,1152]{1,0:T(8,128)S(1)} %copy-done.4, bf16[1024,1152]{1,0:T(8,128)(2,1)} %finish.2.refs_0_), custom_call_target="tpu_custom_call", output_to_operand_aliasing={{}: (4, {})} | custom-call | flops 679477248 | bytes 4000000 | tf_op jit(solution)/shard_map/finish/pallas_call | solution.py:159
  (17 shorter events, 0.0 us)
Async XLA Ops:
  0.0 0.8 copy-start.3
  0.8 2.1 %copy-start.5 = (bf16[1152,1728]{0,1:T(8,128)(2,1)S(1)}, bf16[1152,1728]{0,1:T(8,128)(2,1)}, u32[]{:S(2)}) copy-start(bf16[1152,1728]{0,1:T(8,128)(2,1)} %param.7) | copy-start | bytes 11943940
  2.9 1.7 %copy-start.8 = (bf16[1,1024,1152]{2,1,0:T(8,128)(2,1)S(1)}, bf16[1,1024,1152]{2,1,0:T(8,128)(2,1)}, u32[]{:S(2)}) copy-start(bf16[1,1024,1152]{2,1,0:T(8,128)(2,1)} %param.6) | copy-start | bytes 7077892
  4.6 6.6 %copy-start.4 = (f32[6,1152]{1,0:T(8,128)S(1)}, f32[6,1152]{1,0:T(8,128)}, u32[]{:S(2)}) copy-start(f32[6,1152]{1,0:T(8,128)} %mod_ref.13) | copy-start | bytes 82948
  4.6 6.6 %copy-start.10 = (bf16[576,1152]{1,0:T(8,128)(2,1)S(1)}, bf16[576,1152]{1,0:T(8,128)(2,1)}, u32[]{:S(2)}) copy-start(bf16[576,1152]{1,0:T(8,128)(2,1)} %w_out_ref.5) | copy-start | bytes 3981316
  11.2 15.6 %copy-start.11 = (bf16[1024,1728]{1,0:T(8,128)(2,1)}, bf16[1024,1728]{1,0:T(8,128)(2,1)S(1)}, u32[]{:S(2)}) copy-start(bf16[1024,1728]{1,0:T(8,128)(2,1)S(1)} %project.1.query_ref.triple_ref) | copy-start | bytes 10616836
  26.8 35.3 %all-to-all-start.2 = ((bf16[16,32,1152]{2,1,0:T(8,128)(2,1)}), bf16[16,32,1152]{2,1,0:T(8,128)(2,1)S(1)}, u32[]{:S(2)}, u32[]{:S(2)}) async-start(bf16[16,32,1152]{2,1,0:T(8,128)(2,1)} %bitcast.5), calls=%async_computation.2 | async-start | bytes 2359296 | tf_op jit(solution)/shard_map/all_to_all | solution.py:179
  35.2 1.7 %copy-start.9 = (bf16[1,1024,1152]{2,1,0:T(8,128)(2,1)S(1)}, bf16[1,1024,1152]{2,1,0:T(8,128)(2,1)}, u32[]{:S(2)}) copy-start(bf16[1,1024,1152]{2,1,0:T(8,128)(2,1)} %param.6) | copy-start | bytes 7077892
  36.9 2.0 %copy-start.12 = (bf16[1024,1728]{1,0:T(8,128)(2,1)S(1)}, bf16[1024,1728]{1,0:T(8,128)(2,1)}, u32[]{:S(2)}) copy-start(bf16[1024,1728]{1,0:T(8,128)(2,1)} %copy-done.11) | copy-start | bytes 10616836
  62.1 32.0 %all-to-all-start = ((bf16[16,32,1152]{2,1,0:T(8,128)(2,1)}), bf16[16,32,1152]{2,1,0:T(8,128)(2,1)S(1)}, u32[]{:S(2)}, u32[]{:S(2)}) async-start(bf16[16,32,1152]{2,1,0:T(8,128)(2,1)} %bitcast.2), calls=%async_computation | async-start | bytes 2359296 | tf_op jit(solution)/shard_map/all_to_all | solution.py:179
  68.3 2.1 %copy-start.6 = (bf16[1152,1728]{0,1:T(8,128)(2,1)S(1)}, bf16[1152,1728]{0,1:T(8,128)(2,1)}, u32[]{:S(2)}) copy-start(bf16[1152,1728]{0,1:T(8,128)(2,1)} %param.9) | copy-start | bytes 11943940
  94.1 1.0 copy-start.1
  95.1 22.6 %all-to-all-start.3 = ((bf16[16,32,576]{2,1,0:T(8,128)(2,1)}), bf16[16,32,576]{2,1,0:T(8,128)(2,1)S(1)}, u32[]{:S(2)}, u32[]{:S(2)}) async-start(bf16[16,32,576]{2,1,0:T(8,128)(2,1)} %time.3), calls=%async_computation.3 | async-start | bytes 1310720 | tf_op jit(solution)/shard_map/all_to_all | solution.py:179
  101.2 1.3 copy-start.2
  102.5 2.1 %copy-start.7 = (bf16[1152,1728]{0,1:T(8,128)(2,1)S(1)}, bf16[1152,1728]{0,1:T(8,128)(2,1)}, u32[]{:S(2)}) copy-start(bf16[1152,1728]{0,1:T(8,128)(2,1)} %param.9) | copy-start | bytes 11943940
  104.6 17.7 %copy-start = (bf16[576,1152]{1,0:T(8,128)(2,1)S(1)}, bf16[576,1152]{1,0:T(8,128)(2,1)}, u32[]{:S(2)}) copy-start(bf16[576,1152]{1,0:T(8,128)(2,1)} %w_out_ref.7) | copy-start | bytes 3981316
  117.7 21.0 %all-to-all-start.1 = ((bf16[16,32,576]{2,1,0:T(8,128)(2,1)}), bf16[16,32,576]{2,1,0:T(8,128)(2,1)S(1)}, u32[]{:S(2)}, u32[]{:S(2)}) async-start(bf16[16,32,576]{2,1,0:T(8,128)(2,1)} %time.2), calls=%async_computation.1 | async-start | bytes 1310720 | tf_op jit(solution)/shard_map/all_to_all | solution.py:179
where the time goes:
time: 143 us; the launch traced here: 142 us
  Pallas kernels  65.4 us (46%)
  waiting for transfers between devices  36.2 us (25%)
  starting transfers between devices  25.3 us (18%)
  local copies, waits for them, and re-layouts  14.8 us (10%)
    all_to_all x4, waiting for transfers between devices, exchange(): return lax.all_to_all(array, 'seq', split_axis=0, concat_axis=0, tiled=True)  36.2 us
    pallas_call x2, Pallas kernels, space_chunk(): pl.pallas_call(space_kernel, grid=(steps,), in_specs=[pl.BlockSpec((ROWS,...  31 us
    all_to_all x4, starting transfers between devices, exchange(): return lax.all_to_all(array, 'seq', split_axis=0, concat_axis=0, tiled=True)  25.3 us
    pallas_call x2, Pallas kernels, time_chunk(): pl.pallas_call(time_kernel, grid=(positions // some,), in_specs=[pl.Block...  21.4 us
    unnamed x26, local copies, waits for them, and re-layouts  14.8 us
    pallas_call x1, Pallas kernels, project(): pl.pallas_call(project_kernel, grid=(tokens // ROWS,), in_specs=[pl.Block...  6.62 us
    pallas_call x2, Pallas kernels, finish_chunk(): pl.pallas_call(finish_kernel, grid=(steps,), in_specs=[pl.BlockSpec((ROWS...  6.4 us
  transfers between devices with their start and end apart: 4, of which 4 were waited for; matrix products, arithmetic and copies ran while one was open for 0% of the time, Pallas kernels for 28%

commit v1 on v0

--- a/solution.py
+++ b/solution.py
@@ -59,14 +59,22 @@
             triple_ref[:, head_columns(1, head)],
             triple_ref[:, head_columns(2, head)],
         )
-    delta = jnp.dot(heads_ref[...], w_out_ref[...], preferred_element_type=jnp.float32)
-    out_ref[...] = (rows_ref[...].astype(jnp.float32) + mod_ref[2] * delta).astype(jnp.bfloat16)
-
-
-def time_kernel(rows_ref, w_ref, mod_ref, out_ref, triple_ref, heads_ref):
+    out_ref[...] = gated(rows_ref[...], heads_ref[...], w_out_ref[...], mod_ref[2])
+
+
+def gated(rows, heads, w_out, gate):
+    delta = jnp.dot(heads, w_out, preferred_element_type=jnp.float32)
+    return (rows.astype(jnp.float32) + gate * delta).astype(jnp.bfloat16)
+
+
+def time_kernel(rows_ref, w_ref, mod_ref, *refs):
+    out_ref, triple_ref, heads_ref = refs[-3:]
     members, positions, width = rows_ref.shape
     tokens = members * positions
     rows = rows_ref[...].astype(jnp.float32).reshape(tokens, width)
+    if len(refs) > 3:
+        heads = refs[0][...].astype(jnp.float32).reshape(tokens, INNER).astype(jnp.bfloat16)
+        rows = gated(rows, heads, refs[1][...], mod_ref[2])
     triple_ref[...] = rows_by_columns(mixed_rows(rows, mod_ref[...], 3), w_ref[...])
     left = lax.broadcasted_iota(jnp.int32, (tokens, tokens), 0)
     right = lax.broadcasted_iota(jnp.int32, (tokens, tokens), 1)
@@ -83,8 +91,7 @@
 
 
 def finish_kernel(rows_ref, heads_ref, w_out_ref, mod_ref, *refs):
-    delta = jnp.dot(heads_ref[...], w_out_ref[...], preferred_element_type=jnp.float32)
-    refs[-1][...] = (rows_ref[...].astype(jnp.float32) + mod_ref[5] * delta).astype(jnp.bfloat16)
+    refs[-1][...] = gated(rows_ref[...], heads_ref[...], w_out_ref[...], mod_ref[5])
 
 
 def whole(array):
@@ -124,31 +131,37 @@
             whole(w_out),
             whole(modulation),
         ],
-        out_specs=pl.BlockSpec((ROWS, width), lambda i: (i, 0)),
-        out_shape=jax.ShapeDtypeStruct((block, width), jnp.bfloat16),
-        scratch_shapes=[pltpu.VMEM((ROWS, INNER), jnp.bfloat16)],
+        out_specs=[pl.BlockSpec((ROWS, width), lambda i: (i, 0)), pl.BlockSpec((ROWS, INNER), lambda i: (i, 0))],
+        out_shape=[
+            jax.ShapeDtypeStruct((block, width), jnp.bfloat16),
+            jax.ShapeDtypeStruct((block, INNER), jnp.bfloat16),
+        ],
         compiler_params=params(),
         cost_estimate=pl.CostEstimate(flops=6 * block * tokens * 256 * HEADS, transcendentals=HEADS * block * tokens, bytes_accessed=6000000),
         name="space",
     )(frame, triple, triple, w_out, modulation)
 
 
-def time_chunk(patches, w_t, modulation, members):
+def time_chunk(patches, w_t, modulation, members, heads_in=None, w_out=None):
     tokens, width = patches.shape
     positions = tokens // members
     some = min(positions, max(8, ROWS // members))
     columns = w_t.shape[0]
+    more, specs = [], []
+    if heads_in is not None:
+        more = [heads_in.reshape(members, positions, INNER), w_out]
+        specs = [pl.BlockSpec((members, some, INNER), lambda i: (0, i, 0)), whole(w_out)]
     heads = pl.pallas_call(
         time_kernel,
         grid=(positions // some,),
-        in_specs=[pl.BlockSpec((members, some, width), lambda i: (0, i, 0)), whole(w_t), whole(modulation)],
+        in_specs=[pl.BlockSpec((members, some, width), lambda i: (0, i, 0)), whole(w_t), whole(modulation)] + specs,
         out_specs=pl.BlockSpec((members, some, INNER), lambda i: (0, i, 0)),
         out_shape=jax.ShapeDtypeStruct((members, positions, INNER), jnp.bfloat16),
         scratch_shapes=[pltpu.VMEM((members * some, columns), jnp.bfloat16), pltpu.VMEM((members * some, INNER), jnp.bfloat16)],
         compiler_params=params(),
         cost_estimate=pl.CostEstimate(flops=4 * tokens * width * columns, transcendentals=HEADS * tokens * tokens, bytes_accessed=5000000),
         name="time",
-    )(patches.reshape(members, positions, width), w_t, modulation)
+    )(patches.reshape(members, positions, width), w_t, modulation, *more)
     return heads.reshape(tokens, INNER)
 
 
@@ -182,13 +195,17 @@
 def shards(latent, w_qkv_space, w_out_space, w_qkv_time, w_out_time, modulation):
     members = lax.axis_size("seq")
     frame = latent[0]
+    early = exchange(frame[frame.shape[0] // CHUNKS :])
     triple = project(frame, w_qkv_space.T, modulation)
-    rows = [space_chunk(frame, triple, w_out_space, modulation, chunk) for chunk in range(CHUNKS)]
-    patches = [exchange(part) for part in rows]
-    heads = [exchange(time_chunk(part, w_qkv_time.T, modulation, members)) for part in patches]
-    done = None
-    for chunk in range(CHUNKS):
-        done = finish_chunk(rows[chunk], heads[chunk], w_out_time, modulation, chunk, done)
+    first, _ = space_chunk(frame, triple, w_out_space, modulation, 0)
+    first, early = lax.optimization_barrier((first, early))
+    patches = exchange(first)
+    second, heads = space_chunk(frame, triple, w_out_space, modulation, 1)
+    heads = exchange(heads)
+    first_back = exchange(time_chunk(patches, w_qkv_time.T, modulation, members))
+    second_back = exchange(time_chunk(early, w_qkv_time.T, modulation, members, heads, w_out_space))
+    done = finish_chunk(first, first_back, w_out_time, modulation, 0, None)
+    done = finish_chunk(second, second_back, w_out_time, modulation, 1, done)
     return done[None]
 
 

time: 143 us -> 143 us (level)
  waiting for transfers between devices: 36.2 us -> 21.3 us
  local copies, waits for them, and re-layouts: 14.8 us -> 23.8 us
  starting transfers between devices: 25.3 us -> 32.8 us
  Pallas kernels: 65.4 us -> 63.6 us
    all_to_all x4 -> x5, waiting for transfers between devices: 36.2 us -> 21.3 us  [exchange(): return lax.all_to_all(array, 'seq', split_axis=0, concat_axis=0, tiled=True)]
    all_to_all x4 -> x5, starting transfers between devices: 25.3 us -> 32.8 us  [exchange(): return lax.all_to_all(array, 'seq', split_axis=0, concat_axis=0, tiled=True)]
    unnamed x26 -> x42, local copies, waits for them, and re-layouts: 14.8 us -> 21.4 us
    slice x0 -> x1, local copies, waits for them, and re-layouts: none -> 2.37 us  [shards(): early = exchange(frame[frame.shape[0] // CHUNKS:])]
  transfers between devices with their start and end apart: 4 -> 5, of which waited for: 4 -> 3; matrix products, arithmetic and copies ran while one was open for 0% -> 0% of each run, Pallas kernels for 28% -> 43%
where the time goes in v1:
time: 143 us; the launch traced here: 142 us
  Pallas kernels  63.6 us (44%)
  starting transfers between devices  32.8 us (23%)
  local copies, waits for them, and re-layouts  23.8 us (17%)
  waiting for transfers between devices  21.3 us (15%)
    all_to_all x5, starting transfers between devices, exchange(): return lax.all_to_all(array, 'seq', split_axis=0, concat_axis=0, tiled=True)  32.8 us
    pallas_call x2, Pallas kernels, space_chunk(): pl.pallas_call(space_kernel, grid=(steps,), in_specs=[pl.BlockSpec((ROWS,...  30.2 us
    pallas_call x2, Pallas kernels, time_chunk(): pl.pallas_call(time_kernel, grid=(positions // some,), in_specs=[pl.Block...  21.5 us
    unnamed x42, local copies, waits for them, and re-layouts  21.4 us
    all_to_all x5, waiting for transfers between devices, exchange(): return lax.all_to_all(array, 'seq', split_axis=0, concat_axis=0, tiled=True)  21.3 us
    pallas_call x1, Pallas kernels, project(): pl.pallas_call(project_kernel, grid=(tokens // ROWS,), in_specs=[pl.Block...  6.63 us
    pallas_call x2, Pallas kernels, finish_chunk(): pl.pallas_call(finish_kernel, grid=(steps,), in_specs=[pl.BlockSpec((ROWS...  5.31 us
  transfers between devices with their start and end apart: 5, of which 3 were waited for; matrix products, arithmetic and copies ran while one was open for 0% of the time, Pallas kernels for 43%

profile of v1, /device:TPU:0, one launch (start us, length us, event | category | flops | bytes accessed | tf_op | source)
XLA Modules:
  0.0 141.6 jit_solution(4064842362588057367)
XLA Ops:
  0.0 2.4 %slice.4 = bf16[1,512,1152]{2,1,0:T(8,128)(2,1)} slice(bf16[1,1024,1152]{2,1,0:T(8,128)(2,1)} %param.6), slice={[0:1], [512:1024], [0:1152]} | slice | bytes 2359296 | tf_op jit(solution)/shard_map/slice | solution.py:198
  2.4 8.5 %all-to-all-start = ((bf16[16,32,1152]{2,1,0:T(8,128)(2,1)}), bf16[16,32,1152]{2,1,0:T(8,128)(2,1)S(1)}, u32[]{:S(2)}, u32[]{:S(2)}) async-start(bf16[16,32,1152]{2,1,0:T(8,128)(2,1)} %bitcast.20), calls=%async_computation | async-start | bytes 2359296 | tf_op jit(solution)/shard_map/all_to_all | solution.py:192
  11.6 2.1 %copy-done.13 = bf16[1152,1728]{0,1:T(8,128)(2,1)S(1)} copy-done((bf16[1152,1728]{0,1:T(8,128)(2,1)S(1)}, bf16[1152,1728]{0,1:T(8,128)(2,1)}, u32[]{:S(2)}) %copy-start.13) | copy-done | bytes 3981336
  13.8 6.6 %project.1.query_ref.triple_ref = bf16[1024,1728]{1,0:T(8,128)(2,1)S(1)} custom-call(bf16[1024,1152]{1,0:T(8,128)(2,1)S(1)} %bitcast.14, bf16[1728,1152]{1,0:T(8,128)(2,1)S(1)} %bitcast.17, f32[6,1152]{1,0:T(8,128)S(1)} %copy-done.10), custom_call_target="tpu_custom_call" | custom-call | flops 4076863488 | bytes 10000000 | tf_op jit(solution)/shard_map/project/pallas_call | solution.py:108
  20.4 15.6 %space.3 = (bf16[512,1152]{1,0:T(8,128)(2,1)}, bf16[512,576]{1,0:T(8,128)(2,1)}) custom-call(bf16[1024,1152]{1,0:T(8,128)(2,1)S(1)} %bitcast.15, bf16[1024,1728]{1,0:T(8,128)(2,1)S(1)} %project.1.query_ref.triple_ref, bf16[1024,1728]{1,0:T(8,128)(2,1)S(1)} %project.1.query_ref.triple_ref, bf16[576,1152]{1,0:T(8,128)(2,1)S(1)} %copy-done.16, ...), custom_call_target="tpu_custom_call" | custom-call | flops 6442450944 | bytes 6000000 | tf_op jit(solution)/shard_map/space/pallas_call | solution.py:124
  36.0 1.8 %copy-done.19 = bf16[1024,1728]{1,0:T(8,128)(2,1)} copy-done((bf16[1024,1728]{1,0:T(8,128)(2,1)}, bf16[1024,1728]{1,0:T(8,128)(2,1)S(1)}, u32[]{:S(2)}) %copy-start.19) | copy-done | bytes 3538968
  37.8 7.1 %all-to-all-start.3 = ((bf16[16,32,1152]{2,1,0:T(8,128)(2,1)}), bf16[16,32,1152]{2,1,0:T(8,128)(2,1)S(1)}, u32[]{:S(2)}, u32[]{:S(2)}) async-start(bf16[16,32,1152]{2,1,0:T(8,128)(2,1)} %bitcast.8), calls=%async_computation.3 | async-start | bytes 2359296 | tf_op jit(solution)/shard_map/all_to_all | solution.py:192
  45.0 1.7 %copy-done.9 = bf16[1,1024,1152]{2,1,0:T(8,128)(2,1)S(1)} copy-done((bf16[1,1024,1152]{2,1,0:T(8,128)(2,1)S(1)}, bf16[1,1024,1152]{2,1,0:T(8,128)(2,1)}, u32[]{:S(2)}) %copy-start.9) | copy-done | bytes 2359320
  46.6 1.3 copy-done.17
  47.9 2.0 %copy-done.20 = bf16[1024,1728]{1,0:T(8,128)(2,1)S(1)} copy-done((bf16[1024,1728]{1,0:T(8,128)(2,1)S(1)}, bf16[1024,1728]{1,0:T(8,128)(2,1)}, u32[]{:S(2)}) %copy-start.20) | copy-done | bytes 3538968
  50.0 14.6 %space.2 = (bf16[512,1152]{1,0:T(8,128)(2,1)S(1)}, bf16[512,576]{1,0:T(8,128)(2,1)S(1)}) custom-call(bf16[1024,1152]{1,0:T(8,128)(2,1)S(1)} %bitcast.16, bf16[1024,1728]{1,0:T(8,128)(2,1)S(1)} %copy-done.20, bf16[1024,1728]{1,0:T(8,128)(2,1)S(1)} %copy-done.20, bf16[576,1152]{1,0:T(8,128)(2,1)S(1)} %copy-done.17, f32[6,1152]{1,0:T(8,128)S(1)} %copy-done.12), custom_call_target="tpu_custom_call" | custom-call | flops 6442450944 | bytes 6000000 | tf_op jit(solution)/shard_map/space/pallas_call | solution.py:124
  66.5 4.8 %all-to-all-done.3.rows_ref = bf16[16,32,1152]{2,1,0:T(8,128)(2,1)S(1)} async-done(((bf16[16,32,1152]{2,1,0:T(8,128)(2,1)}), bf16[16,32,1152]{2,1,0:T(8,128)(2,1)S(1)}, u32[]{:S(2)}, u32[]{:S(2)}) %all-to-all-start.3) | async-done | bytes 1179680 | tf_op jit(solution)/shard_map/all_to_all | solution.py:192
  71.2 6.2 %all-to-all-start.1 = ((bf16[16,32,576]{2,1,0:T(8,128)(2,1)}), bf16[16,32,576]{2,1,0:T(8,128)(2,1)S(1)}, u32[]{:S(2)}, u32[]{:S(2)}) async-start(bf16[16,32,576]{2,1,0:T(8,128)(2,1)} %bitcast.13), calls=%async_computation.1 | async-start | bytes 1310720 | tf_op jit(solution)/shard_map/all_to_all | solution.py:192
  77.4 2.1 %copy-done.14 = bf16[1152,1728]{0,1:T(8,128)(2,1)S(1)} copy-done((bf16[1152,1728]{0,1:T(8,128)(2,1)S(1)}, bf16[1152,1728]{0,1:T(8,128)(2,1)}, u32[]{:S(2)}) %copy-start.14) | copy-done | bytes 3981336
  79.5 10.0 %time.3 = bf16[16,32,576]{2,1,0:T(8,128)(2,1)S(1)} custom-call(bf16[16,32,1152]{2,1,0:T(8,128)(2,1)S(1)} %all-to-all-done.3.rows_ref, bf16[1728,1152]{1,0:T(8,128)(2,1)S(1)} %bitcast.18, f32[6,1152]{1,0:T(8,128)S(1)} %copy-done.12), custom_call_target="tpu_custom_call" | custom-call | flops 4076863488 | bytes 5000000 | tf_op jit(solution)/shard_map/time/pallas_call | solution.py:154
  90.3 3.5 %all-to-all-done.1.refs_0_ = bf16[16,32,576]{2,1,0:T(8,128)(2,1)S(1)} async-done(((bf16[16,32,576]{2,1,0:T(8,128)(2,1)}), bf16[16,32,576]{2,1,0:T(8,128)(2,1)S(1)}, u32[]{:S(2)}, u32[]{:S(2)}) %all-to-all-start.1) | async-done | bytes 589856 | tf_op jit(solution)/shard_map/all_to_all | solution.py:192
  93.9 4.2 %all-to-all-start.4 = ((bf16[16,32,576]{2,1,0:T(8,128)(2,1)}), bf16[16,32,576]{2,1,0:T(8,128)(2,1)S(1)}, u32[]{:S(2)}, u32[]{:S(2)}) async-start(bf16[16,32,576]{2,1,0:T(8,128)(2,1)} %copy-done.7), calls=%async_computation.4 | async-start | bytes 1310720 | tf_op jit(solution)/shard_map/all_to_all | solution.py:192
  99.3 2.1 %copy-done.15 = bf16[1152,1728]{0,1:T(8,128)(2,1)S(1)} copy-done((bf16[1152,1728]{0,1:T(8,128)(2,1)S(1)}, bf16[1152,1728]{0,1:T(8,128)(2,1)}, u32[]{:S(2)}) %copy-start.15) | copy-done | bytes 3981336
  101.5 1.3 copy-done.18
  102.8 11.5 %time.2 = bf16[16,32,576]{2,1,0:T(8,128)(2,1)S(1)} custom-call(bf16[16,32,1152]{2,1,0:T(8,128)(2,1)S(1)} %copy-done.4, bf16[1728,1152]{1,0:T(8,128)(2,1)S(1)} %bitcast.19, f32[6,1152]{1,0:T(8,128)S(1)} %copy-done.12, bf16[16,32,576]{2,1,0:T(8,128)(2,1)S(1)} %all-to-all-done.1.refs_0_, bf16[576,1152]{1,0:T(8,128)(2,1)S(1)} %copy-done.18), custom_call_target="tpu_custom_call" | custom-call | flops 4076863488 | bytes 5000000 | tf_op jit(solution)/shard_map/time/pallas_call | solution.py:154
  115.1 6.9 %all-to-all-start.2 = ((bf16[16,32,576]{2,1,0:T(8,128)(2,1)}), bf16[16,32,576]{2,1,0:T(8,128)(2,1)S(1)}, u32[]{:S(2)}, u32[]{:S(2)}) async-start(bf16[16,32,576]{2,1,0:T(8,128)(2,1)} %copy-done.5), calls=%async_computation.2 | async-start | bytes 1310720 | tf_op jit(solution)/shard_map/all_to_all | solution.py:192
  122.1 3.2 %finish.2.refs_0_ = bf16[1024,1152]{1,0:T(8,128)(2,1)} custom-call(bf16[512,1152]{1,0:T(8,128)(2,1)} %get-tuple-element.14.rows_ref, bf16[512,576]{1,0:T(8,128)(2,1)S(1)} %bitcast.12, bf16[576,1152]{1,0:T(8,128)(2,1)S(1)} %copy-done, f32[6,1152]{1,0:T(8,128)S(1)} %copy-done.12), custom_call_target="tpu_custom_call" | custom-call | flops 679477248 | bytes 4000000 | tf_op jit(solution)/shard_map/finish/pallas_call | solution.py:172
  125.3 13.0 %all-to-all-done.2 = bf16[16,32,576]{2,1,0:T(8,128)(2,1)S(1)} async-done(((bf16[16,32,576]{2,1,0:T(8,128)(2,1)}), bf16[16,32,576]{2,1,0:T(8,128)(2,1)S(1)}, u32[]{:S(2)}, u32[]{:S(2)}) %all-to-all-start.2) | async-done | bytes 589856 | tf_op jit(solution)/shard_map/all_to_all | solution.py:192
  139.5 2.1 %finish.3 = bf16[1024,1152]{1,0:T(8,128)(2,1)} custom-call(bf16[512,1152]{1,0:T(8,128)(2,1)S(1)} %copy-done.2, bf16[512,576]{1,0:T(8,128)(2,1)S(1)} %bitcast.11, bf16[576,1152]{1,0:T(8,128)(2,1)S(1)} %copy-done, f32[6,1152]{1,0:T(8,128)S(1)} %copy-done.12, bf16[1024,1152]{1,0:T(8,128)(2,1)} %finish.2.refs_0_), custom_call_target="tpu_custom_call", output_to_operand_aliasing={{}: (4, {})} | custom-call | flops 679477248 | bytes 4000000 | tf_op jit(solution)/shard_map/finish/pallas_call | solution.py:172
  (36 shorter events, 6.9 us)
Async XLA Ops:
  2.4 8.5 %copy-start.8 = (bf16[1,1024,1152]{2,1,0:T(8,128)(2,1)S(1)}, bf16[1,1024,1152]{2,1,0:T(8,128)(2,1)}, u32[]{:S(2)}) copy-start(bf16[1,1024,1152]{2,1,0:T(8,128)(2,1)} %param.6) | copy-start | bytes 7077892
  2.4 35.5 %all-to-all-start = ((bf16[16,32,1152]{2,1,0:T(8,128)(2,1)}), bf16[16,32,1152]{2,1,0:T(8,128)(2,1)S(1)}, u32[]{:S(2)}, u32[]{:S(2)}) async-start(bf16[16,32,1152]{2,1,0:T(8,128)(2,1)} %bitcast.20), calls=%async_computation | async-start | bytes 2359296 | tf_op jit(solution)/shard_map/all_to_all | solution.py:192
  11.6 2.1 %copy-start.13 = (bf16[1152,1728]{0,1:T(8,128)(2,1)S(1)}, bf16[1152,1728]{0,1:T(8,128)(2,1)}, u32[]{:S(2)}) copy-start(bf16[1152,1728]{0,1:T(8,128)(2,1)} %param.7) | copy-start | bytes 11943940
  13.8 6.6 %copy-start.11 = (f32[6,1152]{1,0:T(8,128)S(1)}, f32[6,1152]{1,0:T(8,128)}, u32[]{:S(2)}) copy-start(f32[6,1152]{1,0:T(8,128)} %mod_ref.13) | copy-start | bytes 82948
  13.8 6.6 %copy-start.16 = (bf16[576,1152]{1,0:T(8,128)(2,1)S(1)}, bf16[576,1152]{1,0:T(8,128)(2,1)}, u32[]{:S(2)}) copy-start(bf16[576,1152]{1,0:T(8,128)(2,1)} %refs_1_.1) | copy-start | bytes 3981316
  36.0 1.8 %copy-start.19 = (bf16[1024,1728]{1,0:T(8,128)(2,1)}, bf16[1024,1728]{1,0:T(8,128)(2,1)S(1)}, u32[]{:S(2)}) copy-start(bf16[1024,1728]{1,0:T(8,128)(2,1)S(1)} %project.1.query_ref.triple_ref) | copy-start | bytes 10616836
  37.8 7.1 %copy-start.12 = (f32[6,1152]{1,0:T(8,128)S(1)}, f32[6,1152]{1,0:T(8,128)}, u32[]{:S(2)}) copy-start(f32[6,1152]{1,0:T(8,128)} %mod_ref.13) | copy-start | bytes 82948
  37.8 26.8 %copy-start.3 = (bf16[16,32,1152]{2,1,0:T(8,128)(2,1)}, bf16[16,32,1152]{2,1,0:T(8,128)(2,1)S(1)}, u32[]{:S(2)}) copy-start(bf16[16,32,1152]{2,1,0:T(8,128)(2,1)S(1)} %all-to-all-done) | copy-start | bytes 3538948
  37.8 33.4 %all-to-all-start.3 = ((bf16[16,32,1152]{2,1,0:T(8,128)(2,1)}), bf16[16,32,1152]{2,1,0:T(8,128)(2,1)S(1)}, u32[]{:S(2)}, u32[]{:S(2)}) async-start(bf16[16,32,1152]{2,1,0:T(8,128)(2,1)} %bitcast.8), calls=%async_computation.3 | async-start | bytes 2359296 | tf_op jit(solution)/shard_map/all_to_all | solution.py:192
  45.0 1.7 %copy-start.9 = (bf16[1,1024,1152]{2,1,0:T(8,128)(2,1)S(1)}, bf16[1,1024,1152]{2,1,0:T(8,128)(2,1)}, u32[]{:S(2)}) copy-start(bf16[1,1024,1152]{2,1,0:T(8,128)(2,1)} %param.6) | copy-start | bytes 7077892
  46.6 1.3 copy-start.17
  47.9 2.0 %copy-start.20 = (bf16[1024,1728]{1,0:T(8,128)(2,1)S(1)}, bf16[1024,1728]{1,0:T(8,128)(2,1)}, u32[]{:S(2)}) copy-start(bf16[1024,1728]{1,0:T(8,128)(2,1)} %copy-done.19) | copy-start | bytes 10616836
  64.6 1.0 copy-start.1
  65.6 0.9 copy-start.6
  71.2 22.6 %all-to-all-start.1 = ((bf16[16,32,576]{2,1,0:T(8,128)(2,1)}), bf16[16,32,576]{2,1,0:T(8,128)(2,1)S(1)}, u32[]{:S(2)}, u32[]{:S(2)}) async-start(bf16[16,32,576]{2,1,0:T(8,128)(2,1)} %bitcast.13), calls=%async_computation.1 | async-start | bytes 1310720 | tf_op jit(solution)/shard_map/all_to_all | solution.py:192
  77.4 2.1 %copy-start.14 = (bf16[1152,1728]{0,1:T(8,128)(2,1)S(1)}, bf16[1152,1728]{0,1:T(8,128)(2,1)}, u32[]{:S(2)}) copy-start(bf16[1152,1728]{0,1:T(8,128)(2,1)} %param.9) | copy-start | bytes 11943940
  93.9 21.3 %all-to-all-start.4 = ((bf16[16,32,576]{2,1,0:T(8,128)(2,1)}), bf16[16,32,576]{2,1,0:T(8,128)(2,1)S(1)}, u32[]{:S(2)}, u32[]{:S(2)}) async-start(bf16[16,32,576]{2,1,0:T(8,128)(2,1)} %copy-done.7), calls=%async_computation.4 | async-start | bytes 1310720 | tf_op jit(solution)/shard_map/all_to_all | solution.py:192
  98.0 1.3 copy-start.4
  99.3 2.1 %copy-start.15 = (bf16[1152,1728]{0,1:T(8,128)(2,1)S(1)}, bf16[1152,1728]{0,1:T(8,128)(2,1)}, u32[]{:S(2)}) copy-start(bf16[1152,1728]{0,1:T(8,128)(2,1)} %param.9) | copy-start | bytes 11943940
  101.5 1.3 copy-start.18
  102.8 19.3 %copy-start = (bf16[576,1152]{1,0:T(8,128)(2,1)S(1)}, bf16[576,1152]{1,0:T(8,128)(2,1)}, u32[]{:S(2)}) copy-start(bf16[576,1152]{1,0:T(8,128)(2,1)} %w_out_ref.7) | copy-start | bytes 3981316
  114.3 0.9 copy-start.5
  115.1 23.1 %all-to-all-start.2 = ((bf16[16,32,576]{2,1,0:T(8,128)(2,1)}), bf16[16,32,576]{2,1,0:T(8,128)(2,1)S(1)}, u32[]{:S(2)}, u32[]{:S(2)}) async-start(bf16[16,32,576]{2,1,0:T(8,128)(2,1)} %copy-done.5), calls=%async_computation.2 | async-start | bytes 1310720 | tf_op jit(solution)/shard_map/all_to_all | solution.py:192
  138.2 1.3 copy-start.2
  (2 other events, 1.6 us)
